TPU v7x, 512 devices: a 4x2x32 block of a 4x8x32 slice. The times are simulated.
512 devices in a mesh: groups: 2 (over y), seq: 32 (over z), sample: 4 (over x), vocab: 2 (over core).
Axes of the slice: x: 4, y: 2, z: 32, core: 2. Of those that a mesh axis runs over, the one named last changes fastest.
The devices are a block of a 4x8x32 slice.
Arguments:
- queries: bfloat16 [16, 2048, 1792], P(('groups', 'sample'), 'seq', 'vocab'), parts along dimension 0, may hold values from -130 to 130
- key_states: bfloat16 [16, 2048, 256], P(('groups', 'sample'), 'seq', 'vocab'), parts along dimension 0, may hold values from -8 to 8
- value_states: bfloat16 [16, 2048, 256], P(('groups', 'sample'), 'seq', 'vocab'), parts along dimension 0, may hold values from -6 to 6
- residual: bfloat16 [16, 2048, 1792], P(('groups', 'sample'), 'seq'), parts along dimension 0, may hold values from -3 to 3
- out_weight: bfloat16 [1792, 1792], P('vocab'), may hold values from -0.5 to 0.5
- norm_gain: float32 [1792], replicated, may hold values from 0.5 to 1.5
- vocab_head: bfloat16 [81920, 1792], P(('seq', 'sample', 'vocab')), may hold values from -21 to 21
- targets: int32 [16, 2048], P(('groups', 'sample')), parts along dimension 0, may hold values from 0 to 81919
- scored_slots: int32 [16, 512], P(('groups', 'sample')), parts along dimension 0, may hold values from -1 to 2047, as said below
- lengths: int32 [16], P(('groups', 'sample')), parts along dimension 0, may hold values from 512 to 2048
- rewards: int32 [16], P(('groups', 'sample')), parts along dimension 0, may hold values from 0 to 4
Outputs:
- token_logprobs: float32 [16, 512], P(('groups', 'sample'), 'seq'), parts along dimension 0
- seq_scores: float32 [16], P(('groups', 'sample')), parts along dimension 0
- advantages: float32 [16], P(('groups', 'sample')), parts along dimension 0
- objective: float32 [2], P('groups'), parts along dimension 0
There are 2 independent parts, one for each index of `groups`. A program takes and returns all parts, laid end to end along the dimension named above; an argument that names none is the same for every part. Nothing has to cross between parts.
Inputs may be any that keep to these rules, and one draw needn't show every extreme that they name: `scored_slots`: slots b * 16 to (b + 1) * 16 - 1 of a completion hold distinct positions of b * 64 to (b + 1) * 64 - 1 in rising order, followed by -1 in unused slots; every completion fills all 16 slots of some block; positions not listed are not scored. Positions from lengths[i] on are padding.
All inputs are finite; a program needn't handle non-finite values.
Results may differ from a plain program's by a relative error of at most 0.0085.
Values may be sent and summed in bfloat16 or wider, within the bound.
A program may use at most 64 MiB of HBM per device.

v0:
```python
import jax
import jax.numpy as jnp
from jax import lax
from jax.sharding import PartitionSpec as P

HD = 128
K = 8


floor_value = -1e30


def side_by_side(arrays, axis, dim, along):
    both = jnp.concatenate(arrays, axis=along)
    whole, at, gathered = (lax.all_gather(both, axis, axis=dim, tiled=True), 0, [])
    for a in arrays:
        gathered.append(lax.slice_in_dim(whole, at, at + a.shape[along], axis=along))
        at += a.shape[along]
    return tuple(gathered)


def sent_to_all(value, axis):
    copies = jnp.broadcast_to(value, (lax.axis_size(axis), *value.shape))
    return lax.all_to_all(copies, axis, split_axis=0, concat_axis=0, tiled=True)


def taken_together(value, axis):
    return sent_to_all(value, axis).astype(jnp.float32).sum(axis=0)


def all_in_one(value, axis):
    leaves = jax.tree.leaves(value)
    turns = sorted(range(len(leaves)), key=lambda k: -leaves[k].size)
    width = (1, *leaves[turns[0]].shape)[-1]
    lines = [
        jnp.pad(leaves[k].reshape(-1), (0, -leaves[k].size % width)).reshape(-1, width)
        for k in turns
    ]
    both, at, found = (lax.all_gather(jnp.concatenate(lines), axis), 0, {})
    for k, line in zip(turns, lines):
        slab = both[:, at : at + len(line)].reshape(len(both), -1)
        found[k] = slab[:, : leaves[k].size].reshape(-1, *leaves[k].shape)
        at += len(line)
    numbers = iter(range(len(leaves)))
    return jax.tree.map(lambda _: found[next(numbers)], value)


def joined(value, axis, combine):
    everything = all_in_one(value, axis)
    initial = jax.tree.map(lambda part: part[0], everything)

    def turn(k, so_far):
        return combine(so_far, jax.tree.map(lambda part: part[k], everything))

    return lax.fori_loop(1, lax.axis_size(axis), turn, initial)


def rms_scale(hidden, norm_gain):
    power = jnp.mean(hidden * hidden, axis=-1, keepdims=True)
    return (hidden * lax.rsqrt(power + 1e-06) * norm_gain).astype(jnp.bfloat16)


def merge_stats(left, right):
    top_score = jnp.maximum(left[0], right[0])
    weight_sum = left[1] * jnp.exp(left[0] - top_score) + right[1] * jnp.exp(right[0] - top_score)
    return (top_score, weight_sum, left[2] + right[2])


def shards(
    queries,
    key_states,
    value_states,
    residual,
    out_weight,
    norm_gain,
    vocab_head,
    targets,
    scored_slots,
    lengths,
    rewards,
):
    sample_count, block_len, query_width = queries.shape
    kv_heads = key_states.shape[2] // HD
    group_size = query_width // HD // kv_heads
    model_width = out_weight.shape[1]
    full_len = targets.shape[1]
    slot_total = scored_slots.shape[1]
    slot_cap = slot_total // lax.axis_size("seq")
    first_pos = lax.axis_index("seq") * block_len
    query_pos = first_pos + jnp.arange(block_len, dtype=jnp.int32)
    query_view = queries.reshape(sample_count, block_len, kv_heads, group_size, HD)
    stat_shape = (sample_count, block_len, kv_heads, group_size)
    pieces = side_by_side((key_states, value_states), "seq", 1, 0)
    top_score = jnp.full(stat_shape, floor_value, jnp.float32)
    piece_len = pieces[0].shape[1]
    key_view = pieces[0].reshape(sample_count, piece_len, kv_heads, HD)
    value_view = pieces[1].reshape(sample_count, piece_len, kv_heads, HD)
    scores = jnp.einsum(
        "srkgd,snkd->srkgn", query_view, key_view, preferred_element_type=jnp.float32
    ) * HD ** (-0.5)
    key_pos = jnp.arange(piece_len, dtype=jnp.int32)
    allowed = (key_pos[None, :] <= query_pos[:, None])[None, :, None, None, :]
    masked = jnp.where(allowed, scores, floor_value)
    new_top = jnp.maximum(top_score, jnp.max(masked, axis=-1))
    weights = jnp.where(allowed, jnp.exp(masked - new_top[..., None]), 0.0)
    weight_sum = jnp.sum(weights, axis=-1)
    update = jnp.einsum(
        "srkgn,snkd->srkgd",
        weights.astype(jnp.bfloat16),
        value_view,
        preferred_element_type=jnp.float32,
    )
    weighted = update
    new_top, weight_sum, weighted = (new_top, weight_sum, weighted)
    safe_sum = jnp.where(weight_sum > 0, weight_sum, 1.0)
    attended = (
        (weighted / safe_sum[..., None])
        .reshape(sample_count, block_len, query_width)
        .astype(jnp.bfloat16)
    )
    own_slots = lax.dynamic_slice_in_dim(
        scored_slots, lax.axis_index("seq") * slot_cap, slot_cap, 1
    )
    local_pos = jnp.clip(own_slots - first_pos, 0, block_len - 1)
    picked_attended = jnp.take_along_axis(attended, local_pos[:, :, None], axis=1)
    picked_resid = jnp.take_along_axis(residual, local_pos[:, :, None], axis=1)
    partial_value = jnp.einsum(
        "scq,qd->scd", picked_attended, out_weight, preferred_element_type=jnp.float32
    )
    head_rows = lax.all_gather(vocab_head, "sample", axis=0, tiled=True)
    shard_rows = vocab_head.shape[0]
    row_index = jnp.arange(head_rows.shape[0], dtype=jnp.int32)
    owner = (
        lax.axis_index("seq") * lax.axis_size("sample") + row_index // shard_rows
    ) * lax.axis_size("vocab") + lax.axis_index("vocab")
    vocab_ids = owner * shard_rows + row_index % shard_rows
    summed = taken_together(partial_value.astype(jnp.bfloat16), "vocab").astype(jnp.float32)
    normed = rms_scale(picked_resid.astype(jnp.float32) + summed, norm_gain)
    pieces = lax.all_gather(normed, "seq", axis=1, tiled=True)
    piece_len = pieces.shape[1]
    flat = pieces.reshape(sample_count * piece_len, model_width)
    logits = lax.dot_general(
        flat, head_rows, (((1,), (1,)), ((), ())), preferred_element_type=jnp.float32
    )
    logits = logits.reshape(sample_count, piece_len, head_rows.shape[0])
    top_local = jnp.max(logits, axis=-1)
    sum_local = jnp.sum(jnp.exp(logits - top_local[..., None]), axis=-1)
    slot_piece = jnp.maximum(scored_slots, 0)
    wanted = jnp.take_along_axis(targets, slot_piece, axis=1)
    picked = jnp.sum(jnp.where(vocab_ids[None, None, :] == wanted[..., None], logits, 0.0), axis=-1)
    top_local, sum_local, pick_local = (top_local, sum_local, picked)
    top_all, sum_all, pick_all = joined(
        (top_local, sum_local, pick_local), ("seq", "vocab"), merge_stats
    )
    logprob = pick_all - (top_all + jnp.log(sum_all))
    scored = (scored_slots >= 0) & (scored_slots < lengths[:, None])
    token_all = jnp.where(scored, logprob, 0.0)
    own_scores = jnp.sum(token_all, axis=-1) / full_len
    own_tokens = lax.dynamic_slice_in_dim(token_all, lax.axis_index("seq") * slot_cap, slot_cap, 1)
    own_reward = rewards.astype(jnp.float32)
    reward_all, score_all = (
        lax.all_gather(own_reward, "sample", axis=0, tiled=True),
        lax.all_gather(own_scores, "sample", axis=0, tiled=True),
    )
    reward_sum = jnp.sum(reward_all)
    own_advantage = own_reward - (reward_sum - own_reward) / (K - 1)
    every_advantage = reward_all - (reward_sum - reward_all) / (K - 1)
    objective = -(jnp.sum(every_advantage * score_all) / K).reshape(1)
    return (own_tokens, own_scores, own_advantage, objective)


def solution(mesh):
    in_specs = (
        P(("groups", "sample"), "seq", "vocab"),
        P(("groups", "sample"), "seq", "vocab"),
        P(("groups", "sample"), "seq", "vocab"),
        P(("groups", "sample"), "seq", None),
        P("vocab", None),
        P(),
        P(("seq", "sample", "vocab"), None),
        P(("groups", "sample"), None),
        P(("groups", "sample"), None),
        P(("groups", "sample")),
        P(("groups", "sample")),
    )
    out_specs = (
        P(("groups", "sample"), "seq"),
        P(("groups", "sample")),
        P(("groups", "sample")),
        P("groups"),
    )
    return jax.shard_map(shards, mesh=mesh, in_specs=in_specs, out_specs=out_specs, check_vma=False)
```

profile of v0, /device:TPU:40, one launch (start us, length us, event | category | flops | bytes accessed | tf_op | source)
XLA Modules:
  0.0 512.0 jit_solution(15304321632450815917)
XLA Ops:
  7.3 1.5 pad_maximum_fusion
  9.8 0.8 compare_and_fusion
  10.6 2.6 gather_fusion
  13.4 157.4 %all-gather.6.cloned.1.call-done = bf16[4,2048,128]{2,1,0:T(8,128)(2,1)} async-done(((bf16[4,64,128]{2,1,0:T(8,128)(2,1)}), bf16[4,2048,128]{2,1,0:T(8,128)(2,1)}) %all-gather.6.cloned.1.call-update) | async-done | bytes 2097168 | tf_op jit(solution)/shard_map/all_gather | solution.py:15
  170.8 2.7 fusion.2
  173.5 2.2 fusion.3
  175.7 1.6 fusion.26
  177.3 0.9 copy.21
  178.2 1.2 convert_element_type.31
  179.4 0.8 gather_fusion.1
  180.9 3.9 all_to_all.5
  185.1 0.8 multiply_convert_fusion
  186.0 9.1 %gather_fusion.2 = s32[1024]{0:T(1024)S(1)} fusion(s32[2,2048]{1,0:T(2,128)S(1)} %copy-done.1, s32[1024]{0:T(1024)S(1)} %bitcast.125), kind=kCustom, calls=%fused_computation.2 | custom fusion | bytes 16384 | tf_op jit(solution)/shard_map/jit(take_along_axis)/gather | solution.py:149
  195.1 1.3 dynamic-slice
  197.2 34.9 %all-gather.10.cloned.1.call-done = bf16[1280,1792]{1,0:T(8,128)(2,1)} async-done(((bf16[320,1792]{1,0:T(8,128)(2,1)}), bf16[1280,1792]{1,0:T(8,128)(2,1)}) %all-gather.10.cloned.1.call-update) | async-done | bytes 4587536 | tf_op jit(solution)/shard_map/all_gather | solution.py:130
  232.1 142.7 %all-gather.8.cloned.1.call-done = bf16[2,512,1792]{2,1,0:T(8,128)(2,1)} async-done(((bf16[2,16,1792]{2,1,0:T(8,128)(2,1)}), bf16[2,512,1792]{2,1,0:T(8,128)(2,1)}) %all-gather.8.cloned.1.call-update) | async-done | bytes 3670032 | tf_op jit(solution)/shard_map/all_gather | solution.py:139
  374.7 8.5 %fusion.54 = (f32[2,512]{1,0:T(2,128)S(1)}, f32[2,512,1280]{2,1,0:T(8,128)S(1)}) fusion(bf16[2,512,1792]{2,1,0:T(8,128)(2,1)} %all-gather.8.cloned.1.call-done, bf16[1280,1792]{1,0:T(8,128)(2,1)} %all-gather.10.cloned.1.call-done), kind=kOutput, calls=%fused_computation.86 | convolution fusion | flops 4698930176 | bytes 13504512 | tf_op jit(solution)/shard_map/dot_general | solution.py:142
  383.2 1.5 exponential_reduce_fusion
  384.8 57.0 %all-gather.1 = f32[64,6,512]{2,1,0:T(8,128)S(1)} all-gather(f32[1,6,512]{2,1,0:T(8,128)S(1)} %maximum_bitcast_fusion), channel_id=2, replica_groups=mesh['groups'=2,'seq'=32,'sample'=4,'vocab'=2] {'seq','vocab'}, dimensions={0}, use_global_device_ids=true | all-gather | bytes 798720 | tf_op jit(solution)/shard_map/all_gather | solution.py:39
  441.7 1.1 fusion.53
  442.8 46.1 %while.19 = (s32[]{:T(128)}, f32[2,512]{1,0:T(2,128)S(1)}, f32[2,512]{1,0:T(2,128)S(1)}, f32[2,512]{1,0:T(2,128)S(1)}, f32[64,2,512]{2,1,0:T(2,128)}, /*index=5*...) while((s32[]{:T(128)}, f32[2,512]{1,0:T(2,128)S(1)}, ...), condition=%wide.region_8.9_spmd, body=%wide.region_7.8_spmd.sunk | while | flops 7173 | bytes 37011 | solution.py:55
  489.7 10.3 %all-reduce.2 = (f32[8]{0:T(128)S(1)}, f32[8]{0:T(128)S(1)}) all-reduce(f32[8]{0:T(128)S(1)} %convert_dynamic-update-slice_fusion, f32[8]{0:T(128)S(1)} %get-tuple-element.205), channel_id=1, replica_groups=mesh['groups'=2,'seq'=32,'sample'=4,'vocab'=2] {'sample'}, use_global_device_ids=true, to_apply=%add | all-reduce | flops 16 | bytes 128
  500.6 1.2 multiply_subtract_fusion
  501.8 1.2 multiply_reduce_fusion.1
  (110 shorter events, 49.5 us)
Async XLA Ops:
  7.2 173.1 %copy-start = (bf16[896,1792]{1,0:T(8,128)(2,1)S(1)}, bf16[896,1792]{1,0:T(8,128)(2,1)}, u32[]{:S(2)}) copy-start(bf16[896,1792]{1,0:T(8,128)(2,1)} %param.17) | copy-start | bytes 9633796
  7.2 163.6 %all-gather.6.cloned.1.call-start = ((), (), s32[]{:S(2)}) async-start(), calls=%async_computation.1 | async-start | bytes 2162688 | tf_op jit(solution)/shard_map/all_gather | solution.py:15
  8.9 223.2 %all-gather.10.cloned.1.call-start = ((), (), s32[]{:S(2)}) async-start(), calls=%async_computation.3 | async-start | bytes 5734400 | tf_op jit(solution)/shard_map/all_gather | solution.py:130
  9.7 365.0 %all-gather.8.cloned.1.call-start = ((), (), s32[]{:S(2)}) async-start(), calls=%async_computation.2 | async-start | bytes 3784704 | tf_op jit(solution)/shard_map/all_gather | solution.py:139
  173.5 2.3 copy-start.3
  177.3 7.8 %copy-start.5 = (f32[1792]{0:T(1024)S(1)}, f32[1792]{0:T(1024)}, u32[]{:S(2)}) copy-start(f32[1792]{0:T(1024)} %param.18) | copy-start | bytes 21508
  177.3 8.6 %copy-start.4 = (s32[2,512]{1,0:T(2,128)S(1)}, s32[2,512]{1,0:T(2,128)}, u32[]{:S(2)}) copy-start(s32[2,512]{1,0:T(2,128)} %param.21) | copy-start | bytes 12292
  177.3 8.6 %copy-start.1 = (s32[2,2048]{1,0:T(2,128)S(1)}, s32[2,2048]{1,0:T(2,128)}, u32[]{:S(2)}) copy-start(s32[2,2048]{1,0:T(2,128)} %param.20) | copy-start | bytes 49156
  180.3 4.6 copy-start.2
  180.3 16.8 %copy-start.7 = (s32[2]{0:T(128)S(1)}, s32[2]{0:T(128)}, u32[]{:S(2)}) copy-start(s32[2]{0:T(128)} %param.23) | copy-start | bytes 28
  383.2 105.7 %copy-start.6 = (s32[2]{0:T(128)S(1)}, s32[2]{0:T(128)}, u32[]{:S(2)}) copy-start(s32[2]{0:T(128)} %param.22) | copy-start | bytes 28
Sparse Core Ops, SparseCore 0:
  10.1 160.6 all-gather.5
  172.9 59.0 all-gather.9
  234.2 140.4 all-gather.7
where the time goes:
time: 517 us; the launch traced here: 512 us
  waiting for transfers between devices  336 us (65%)
  blocking collectives  71.2 us (14%)
  other arithmetic  56.3 us (11%)
  local copies, waits for them, and re-layouts  17.8 us (3%)
  between operations  16.5 us (3%)
  matrix products  13.3 us (3%)
    all_gather x1, waiting for transfers between devices, side_by_side(): lax.all_gather(both, axis, axis=dim, tiled=True)  157 us
    all_gather x1, waiting for transfers between devices, shards(): pieces = lax.all_gather(normed, 'seq', axis=1, tiled=True)  143 us
    all_gather x1, blocking collectives, all_in_one(): both, at, found = (lax.all_gather(jnp.concatenate(lines), axis), 0, {})  57 us
    add x63, other arithmetic, merge_stats(): left[1] * jnp.exp(left[0] - top_score)  45.2 us
    all_gather x1, waiting for transfers between devices, shards(): head_rows = lax.all_gather(vocab_head, 'sample', axis=0, tiled=True)  34.9 us
  transfers between devices with their start and end apart: 3, of which 3 were waited for; matrix products, arithmetic and copies ran while one was open for 5% of the time, Pallas kernels for 0%

commit v1 on v0

v1 whole, which is shorter than its diff:
```python
import functools

import jax
import jax.numpy as jnp
from jax import lax
from jax.experimental import pallas as pl
from jax.experimental.pallas import tpu as pltpu
from jax.sharding import PartitionSpec as P

HD = 128
LANES = 128
STEP = 4
FLOOR = -1e30
NT = (((1,), (1,)), ((), ()))
MESH = pl.DeviceIdType.MESH
F32 = jnp.float32
BF16 = jnp.bfloat16


def kernel(
    nz,
    nx,
    full_len,
    info_ref,
    len_ref,
    rew_ref,
    gain_ref,
    q_hbm,
    k_hbm,
    v_hbm,
    res_hbm,
    w_hbm,
    head_hbm,
    tok_ref,
    seq_ref,
    adv_ref,
    obj_ref,
    q_buf,
    res_buf,
    w_buf,
    head,
    kv,
    nrm,
    q_rows,
    res_rows,
    top_buf,
    sum_buf,
    acc_buf,
    part,
    part_in,
    stat,
    stat_out,
    stat_in,
    line,
    x_in,
    z_out,
    z_in,
    load_sem,
    head_send,
    head_recv,
    kv_send,
    kv_recv,
    nrm_send,
    nrm_recv,
    mate_send,
    mate_recv,
    part_send,
    part_recv,
    stat_send,
    stat_recv,
    x_send,
    x_recv,
    z_send,
    z_recv,
):
    z = lax.axis_index("seq")
    x = lax.axis_index("sample")
    c = lax.axis_index("vocab")
    half = nz // 2
    own = nz - 1
    block_len = q_buf.shape[1]
    slots = nrm.shape[2]
    group = q_buf.shape[2] // HD
    width = nrm.shape[3]
    rows = head.shape[1]
    cut = width // 2
    z_up, z_down = lax.rem(z + 1, nz), lax.rem(z + nz - 1, nz)
    mate = {"vocab": 1 - c}

    def up(s):
        return (s - 1) // STEP * (2 * STEP) + (s - 1) % STEP

    def down(s):
        return up(s) + STEP

    def send(src, dst, send_sem, recv_sem, where):
        return pltpu.make_async_remote_copy(
            src_ref=src,
            dst_ref=dst,
            send_sem=send_sem,
            recv_sem=recv_sem,
            device_id=where,
            device_id_type=MESH,
        )

    loads = [
        pltpu.make_async_copy(k_hbm, kv.at[own, 0], load_sem.at[0]),
        pltpu.make_async_copy(v_hbm, kv.at[own, 1], load_sem.at[1]),
        pltpu.make_async_copy(head_hbm, head.at[0], load_sem.at[2]),
        pltpu.make_async_copy(q_hbm, q_buf, load_sem.at[3]),
        pltpu.make_async_copy(res_hbm.at[c], res_buf, load_sem.at[4]),
        pltpu.make_async_copy(w_hbm, w_buf, load_sem.at[5]),
    ]
    for load in loads:
        load.start()
    barrier = pltpu.get_barrier_semaphore()
    peers = [{"seq": z_up}, {"seq": z_down}, mate]
    peers += [{"sample": lax.rem(x + d, nx)} for d in range(1, nx)]
    for peer in peers:
        pl.semaphore_signal(barrier, inc=1, device_id=peer, device_id_type=MESH)
    pl.semaphore_wait(barrier, len(peers))

    def kv_copy(src, dst, part_no, where):
        return send(
            kv.at[src, part_no],
            kv.at[dst, part_no],
            kv_send.at[dst, part_no],
            kv_recv.at[dst, part_no],
            {"seq": where},
        )

    for i in range(2):
        loads[i].wait()
        kv_copy(own, up(1), i, z_up).start()
        kv_copy(own, down(1), i, z_down).start()

    hx = rows // 2
    right, left = {"sample": lax.rem(x + 1, nx)}, {"sample": lax.rem(x + nx - 1, nx)}

    def head_copy(src, dst, lo, n, where):
        return send(
            head.at[src, pl.ds(lo, hx)],
            head.at[dst, pl.ds(lo, hx)],
            head_send.at[n],
            head_recv.at[n],
            where,
        )

    loads[2].wait()
    to_right = [head_copy(0, 3, 0, 0, right), head_copy(0, 3, hx, 1, right)]
    to_left = [head_copy(0, 1, hx, 2, left), head_copy(0, 1, 0, 3, left)]
    pass_right = head_copy(3, 2, 0, 4, right)
    pass_left = head_copy(1, 2, hx, 5, left)
    for a, b in zip(to_right, to_left):
        a.start()
        b.start()

    lane = lax.broadcasted_iota(jnp.int32, (1, LANES), 1)
    own_info = info_ref[z]

    def picker(e):
        wide = jnp.broadcast_to(own_info, (slots, LANES))
        at = lax.broadcasted_iota(jnp.int32, (slots, LANES), 0) + (2 * slots + e * slots)
        spot = jnp.sum(
            jnp.where(lax.broadcasted_iota(jnp.int32, (slots, LANES), 1) == at, wide, 0),
            axis=1,
            keepdims=True,
        )
        local = jnp.clip(spot - z * block_len, 0, block_len - 1)
        hot = lax.broadcasted_iota(jnp.int32, (slots, block_len), 1) == local
        return hot.astype(F32).astype(BF16), local

    picks = [picker(e) for e in range(2)]
    loads[3].wait()
    for e in range(2):
        rows_e = jnp.dot(picks[e][0], q_buf[e], preferred_element_type=F32).astype(BF16)
        for h in range(group):
            q_rows[e, pl.ds(h * slots, slots), :] = rows_e[:, h * HD : (h + 1) * HD]
    loads[4].wait()
    own_pick = jnp.where(c == 0, picks[0][0].astype(F32), picks[1][0].astype(F32)).astype(BF16)
    res_rows[...] = jnp.dot(own_pick, res_buf[...], preferred_element_type=F32)

    scale = HD ** (-0.5)
    for e in range(2):
        s0 = lax.dot_general(q_rows[e], kv[own, 0, e], NT, preferred_element_type=F32) * scale
        spot = jnp.concatenate([picks[e][1]] * group, axis=0)
        ok = lax.broadcasted_iota(jnp.int32, s0.shape, 1) <= spot
        s0 = jnp.where(ok, s0, FLOOR)
        top = jnp.max(s0, axis=1, keepdims=True)
        w0 = jnp.where(ok, jnp.exp(s0 - top), 0.0)
        top_buf[e] = jnp.broadcast_to(top, top_buf.shape[1:])
        sum_buf[e] = jnp.broadcast_to(jnp.sum(w0, axis=1, keepdims=True), sum_buf.shape[1:])
        acc_buf[e] = jnp.dot(w0.astype(BF16), kv[own, 1, e], preferred_element_type=F32)

    def attend(first):
        span = 2 * STEP * block_len
        piece = lax.broadcasted_iota(jnp.int32, (1, span), 1) // block_len
        off = first // 2 + 1 + piece % STEP
        is_up = piece < STEP
        ok = jnp.where(is_up, off - z, 1 - jnp.where(off < half, z + off - nz + 1, 0)) <= 0
        for e in range(2):
            keys = kv[pl.ds(first, 2 * STEP), 0, e].reshape(span, HD)
            vals = kv[pl.ds(first, 2 * STEP), 1, e].reshape(span, HD)
            sc = lax.dot_general(q_rows[e], keys, NT, preferred_element_type=F32) * scale
            sc = jnp.where(ok, sc, FLOOR)
            old = top_buf[e][:, :1]
            top = jnp.maximum(old, jnp.max(sc, axis=1, keepdims=True))
            wt = jnp.exp(sc - top)
            fade = jnp.exp(old - top)
            total = sum_buf[e][:, :1] * fade + jnp.sum(wt, axis=1, keepdims=True)
            acc_buf[e] = acc_buf[e] * fade + jnp.dot(
                wt.astype(BF16), vals, preferred_element_type=F32
            )
            top_buf[e] = jnp.broadcast_to(top, top_buf.shape[1:])
            sum_buf[e] = jnp.broadcast_to(total, sum_buf.shape[1:])

    def kv_step(i, carry):
        s = i + 1
        for n in range(2):
            kv_copy(own, up(s), n, z_up).wait_recv()

            @pl.when(s < half)
            def _():
                kv_copy(up(s), up(s + 1), n, z_up).start()
                kv_copy(own, down(s), n, z_down).wait_recv()

            @pl.when(s < half - 1)
            def _():
                kv_copy(down(s), down(s + 1), n, z_down).start()

        @pl.when(s == half // 2)
        def _():
            to_right[0].wait_recv()
            pass_right.start()
            to_left[0].wait_recv()
            pass_left.start()

        @pl.when(s % STEP == 0)
        def _():
            attend((s - 1) // STEP * (2 * STEP))

        return carry

    lax.fori_loop(0, half, kv_step, 0)

    sides = []
    for e in range(2):
        att = (acc_buf[e] / sum_buf[e]).astype(BF16)
        sides.append(
            jnp.concatenate([att[h * slots : (h + 1) * slots] for h in range(group)], axis=1)
        )
    loads[5].wait()
    both = jnp.dot(jnp.concatenate(sides, axis=0), w_buf[...], preferred_element_type=F32)
    for e in range(2):
        part[e] = both[e * slots : (e + 1) * slots]
    swap = send(part.at[1 - c], part_in, part_send, part_recv, mate)
    swap.start()
    hidden = res_rows[...] + part[c]
    swap.wait_recv()
    hidden = hidden + part_in[...]
    power = jnp.mean(hidden * hidden, axis=1, keepdims=True)
    nrm[own, c] = (hidden * lax.rsqrt(power + 1e-06) * gain_ref[...]).astype(BF16)

    def nrm_copy(src, dst, n, where):
        at = pl.ds(n * cut, cut)
        return send(
            nrm.at[src, c, :, at],
            nrm.at[dst, c, :, at],
            nrm_send.at[dst, n],
            nrm_recv.at[dst, n],
            {"seq": where},
        )

    def mate_copy(slot, e):
        return send(nrm.at[slot, e], nrm.at[slot, e], mate_send.at[slot], mate_recv.at[slot], mate)

    for n in range(2):
        nrm_copy(own, up(1), n, z_up).start()
        nrm_copy(own, down(1), n, z_down).start()
    mate_copy(own, c).start()
    to_right[1].wait_recv()
    to_left[1].wait_recv()
    pass_right.wait_recv()
    pass_left.wait_recv()

    def origin(slot):
        s = slot // (2 * STEP) * STEP + slot % STEP + 1
        move = jnp.where(slot % (2 * STEP) < STEP, nz - s, jnp.where(slot == own, 0, s))
        return lax.rem(z + move, nz)

    def scored(first, j):
        batch = nrm[pl.ds(first, 2 * STEP)].reshape(2 * STEP * 2 * slots, width)
        logits = lax.dot_general(head[j], batch, NT, preferred_element_type=F32)
        base = ((z * nx + lax.rem(x + j, nx)) * 2 + c) * rows
        ids = lax.broadcasted_iota(jnp.int32, logits.shape, 0) + base
        want = []
        per = LANES // (2 * slots)
        for t in range(2 * STEP // per):
            lines = info_ref[origin(first + t * per)]
            for i in range(1, per):
                moved = pltpu.roll(info_ref[origin(first + t * per + i)], i * 2 * slots, 1)
                lines = jnp.where(lane < i * 2 * slots, lines, moved)
            want.append(lines)
        want = jnp.concatenate(want, axis=1)
        hit = jnp.sum(jnp.where(ids == want, logits, 0.0), axis=0, keepdims=True)
        fresh = jnp.where(j == 0, 0.0, 1.0)
        old = jnp.where(j == 0, FLOOR, stat[0])
        top = jnp.maximum(old, jnp.max(logits, axis=0, keepdims=True))
        total = jnp.sum(jnp.exp(logits - top), axis=0, keepdims=True)
        stat[0] = top
        stat[1] = jnp.where(j == 0, 0.0, stat[1]) * jnp.exp(old - top) * fresh + total
        stat[2] = jnp.where(j == 0, 0.0, stat[2]) + hit

    me = z * 2 + c

    def stat_copy(slot, to, who):
        return send(
            stat_out.at[slot],
            stat_in.at[me],
            stat_send.at[slot, to],
            stat_recv.at[me],
            {"seq": origin(slot), "vocab": who},
        )

    def give(first):
        per = LANES // (2 * slots)
        for i in range(2 * STEP):
            at = pl.ds(i // per * LANES, LANES)
            back = i % per * 2 * slots
            msg = jnp.zeros((1, LANES), F32)
            for n in range(3):
                got = pltpu.roll(stat[n][:, at.start : at.start + LANES], (LANES + n * 2 * slots - back) % LANES, 1)
                inside = (lane >= n * 2 * slots) & (lane < (n + 1) * 2 * slots)
                msg = jnp.where(inside, got, msg)
            stat_out[first + i] = msg
            if i == 2 * STEP - 1:

                @pl.when(first + i == own)
                def _():
                    stat_in[me] = msg

        for i in range(2 * STEP):
            stat_copy(first + i, 1, 1 - c).start()
            if i < 2 * STEP - 1:
                stat_copy(first + i, 0, c).start()
            else:

                @pl.when(first + i != own)
                def _():
                    stat_copy(first + i, 0, c).start()

    def nrm_step(i, carry):
        s = i + 1

        @pl.when(s <= half)
        def _():
            for n in range(2):
                nrm_copy(own, up(s), n, z_up).wait_recv()

                @pl.when(s < half)
                def _():
                    nrm_copy(up(s), up(s + 1), n, z_up).start()
                    nrm_copy(own, down(s), n, z_down).wait_recv()

                @pl.when(s < half - 1)
                def _():
                    nrm_copy(down(s), down(s + 1), n, z_down).start()

            mate_copy(up(s), c).start()

            @pl.when(s < half)
            def _():
                mate_copy(down(s), c).start()

        @pl.when(s > STEP)
        def _():
            j = (s - 1) % STEP
            first = ((s - 1) // STEP - 1) * (2 * STEP)

            @pl.when(j == 0)
            def _():
                for t in range(2 * STEP):
                    mate_copy(first + t, 1 - c).wait_recv()

            scored(first, j)

            @pl.when(j == STEP - 1)
            def _():
                give(first)

        return carry

    lax.fori_loop(0, half + STEP, nrm_step, 0)

    def stat_wait(k, carry):
        @pl.when(k != me)
        def _():
            send(stat_out.at[0], stat_in.at[k], stat_send.at[0, 0], stat_recv.at[k], mate).wait_recv()

        return carry

    lax.fori_loop(0, 2 * nz, stat_wait, 0)
    two = 2 * slots
    got = stat_in[...]
    m_all = jnp.max(got, axis=0)
    mid = (lane >= two) & (lane < 2 * two)
    m_mid = pltpu.roll(m_all, two, 1)
    sums = jnp.zeros((1, LANES), F32)
    for k in range(2 * nz):
        one = got[k]
        grow = jnp.where(mid, pltpu.roll(one, two, 1) - m_mid, 0.0)
        sums = sums + one * jnp.exp(grow)
    hits = pltpu.roll(sums, LANES - 2 * two, 1)
    exps = pltpu.roll(sums, LANES - two, 1)
    inside = lane < two
    logprob = hits - (m_all + jnp.log(jnp.where(inside, exps, 1.0)))
    spot = pltpu.roll(own_info, LANES - two, 1)
    limit = jnp.where(lane < slots, len_ref[0], len_ref[1])
    ok = inside & (spot >= 0) & (spot < limit)
    tokens = jnp.where(ok, logprob, 0.0)
    tok_ref[0:1, :] = tokens[:, :slots]
    tok_ref[1:2, :] = pltpu.roll(tokens, LANES - slots, 1)[:, :slots]

    r0, r1 = rew_ref[0].astype(F32), rew_ref[1].astype(F32)
    rewards = jnp.where(lane % two < slots, r0, r1)
    mine = jnp.where(inside, tokens, jnp.where(lane < 2 * two, rewards, 0.0))
    line[...] = mine
    x_in[0] = mine

    def x_copy(d):
        where = {"sample": lax.rem(x + d, nx)}
        return send(line, x_in.at[nx - d], x_send.at[d], x_recv.at[nx - d], where)

    for d in range(1, nx):
        x_copy(d).start()
    for d in range(1, nx):
        x_copy(d).wait_recv()
    all_tok = jnp.zeros((1, LANES), F32)
    all_rew = jnp.zeros((1, LANES), F32)
    for k in range(nx):
        d = lax.rem(k + nx - x, nx)
        here = (lane >= k * two) & (lane < (k + 1) * two)
        one = x_in[d]
        all_tok = jnp.where(here, pltpu.roll(one, k * two, 1), all_tok)
        all_rew = jnp.where(here, pltpu.roll(one, (LANES + k * two - two) % LANES, 1), all_rew)
    z_out[...] = all_tok
    z_in[z] = all_tok

    def z_copy(d):
        where = {"seq": lax.rem(z + d, nz)}
        return send(z_out, z_in.at[z], z_send.at[d], z_recv.at[z], where)

    def z_start(d, carry):
        z_copy(d).start()
        return carry

    def z_wait(d, carry):
        k = lax.rem(z + d, nz)
        send(z_out, z_in.at[k], z_send.at[d], z_recv.at[k], {"seq": k}).wait()
        return carry

    lax.fori_loop(1, nz, z_start, 0)

    for n in range(2):
        for k in range(nz - 1):
            kv_copy(own, k, n, z_up).wait_send()
            nrm_copy(own, k, n, z_up).wait_send()
    for k in range(nz):
        mate_copy(k, c).wait_send()
        stat_copy(k, 1, 1 - c).wait_send()
        if k != own:
            stat_copy(k, 0, c).wait_send()
    for copy in to_right + to_left + [pass_right, pass_left, swap]:
        copy.wait_send()
    for d in range(1, nx):
        x_copy(d).wait_send()
    lax.fori_loop(1, nz, z_wait, 0)

    total = jnp.sum(z_in[...], axis=0)
    count = 2 * nx
    reward_sum = jnp.sum(all_rew, axis=1, keepdims=True) / slots
    gain = all_rew - (reward_sum - all_rew) / (count - 1)
    score = total / full_len
    obj_ref[...] = -(jnp.sum(gain * score, axis=1, keepdims=True) / count)
    parts = [
        jnp.sum(jnp.where(lane // slots == 2 * x + e, score, 0.0), axis=1, keepdims=True)
        for e in range(2)
    ]
    advs = [r - (reward_sum - r) / (count - 1) for r in (r0, r1)]
    pair = lax.broadcasted_iota(jnp.int32, (1, 2), 1)
    seq_ref[...] = jnp.where(pair == 0, parts[0], parts[1])
    adv_ref[...] = jnp.where(pair == 0, advs[0], advs[1])


def shards(
    nz,
    nx,
    queries,
    key_states,
    value_states,
    residual,
    out_weight,
    norm_gain,
    vocab_head,
    targets,
    scored_slots,
    lengths,
    rewards,
):
    count, block_len, q_width = queries.shape
    width = out_weight.shape[1]
    rows = vocab_head.shape[0]
    full_len = targets.shape[1]
    slots = scored_slots.shape[1] // nz
    heads = q_width // HD * slots
    spots = scored_slots.reshape(count, nz, slots)
    first = (jnp.arange(nz, dtype=jnp.int32) * block_len)[None, :, None]
    local = jnp.clip(spots - first, 0, block_len - 1)
    hot = local[..., None] == jnp.arange(block_len, dtype=jnp.int32)
    want = jnp.sum(jnp.where(hot, targets.reshape(count, nz, 1, block_len), 0), axis=-1)
    info = jnp.stack([want, spots]).transpose(2, 0, 1, 3).reshape(nz, 1, 2 * count * slots)
    info = jnp.pad(info, ((0, 0), (0, 0), (0, LANES - info.shape[2])))

    vmem, smem, hbm = (
        pl.BlockSpec(memory_space=pltpu.VMEM),
        pl.BlockSpec(memory_space=pltpu.SMEM),
        pl.BlockSpec(memory_space=pl.ANY),
    )
    dma = pltpu.SemaphoreType.DMA
    tokens, scores, advs, objective = pl.pallas_call(
        functools.partial(kernel, nz, nx, full_len),
        out_shape=(
            jax.ShapeDtypeStruct((count, slots), F32),
            jax.ShapeDtypeStruct((1, count), F32),
            jax.ShapeDtypeStruct((1, count), F32),
            jax.ShapeDtypeStruct((1, 1), F32),
        ),
        in_specs=[vmem, smem, smem, vmem] + [hbm] * 6,
        out_specs=(vmem,) * 4,
        scratch_shapes=[
            pltpu.VMEM(queries.shape, BF16),
            pltpu.VMEM(residual.shape[1:], BF16),
            pltpu.VMEM(out_weight.shape, BF16),
            pltpu.VMEM((nx, rows, width), BF16),
            pltpu.VMEM((nz, 2, count, block_len, HD), BF16),
            pltpu.VMEM((nz, count, slots, width), BF16),
            pltpu.VMEM((count, heads, HD), BF16),
            pltpu.VMEM((slots, width), F32),
            pltpu.VMEM((count, heads, HD), F32),
            pltpu.VMEM((count, heads, HD), F32),
            pltpu.VMEM((count, heads, HD), F32),
            pltpu.VMEM((count, slots, width), F32),
            pltpu.VMEM((slots, width), F32),
            pltpu.VMEM((3, 1, 2 * STEP * count * slots), F32),
            pltpu.VMEM((nz, 1, LANES), F32),
            pltpu.VMEM((2 * nz, 1, LANES), F32),
            pltpu.VMEM((1, LANES), F32),
            pltpu.VMEM((nx, 1, LANES), F32),
            pltpu.VMEM((1, LANES), F32),
            pltpu.VMEM((nz, 1, LANES), F32),
            dma((6,)),
            dma((6,)),
            dma((6,)),
            dma((nz, 2)),
            dma((nz, 2)),
            dma((nz, 2)),
            dma((nz, 2)),
            dma((nz,)),
            dma((nz,)),
            dma,
            dma,
            dma((nz, 2)),
            dma((2 * nz,)),
            dma((nx,)),
            dma((nx,)),
            dma((nz,)),
            dma((nz,)),
        ],
        compiler_params=pltpu.CompilerParams(collective_id=0, has_side_effects=True),
    )(
        info,
        lengths,
        rewards,
        norm_gain.reshape(1, width),
        queries,
        key_states,
        value_states,
        residual,
        out_weight,
        vocab_head,
    )
    return (tokens, scores.reshape(count), advs.reshape(count), objective.reshape(1))


def solution(mesh):
    in_specs = (
        P(("groups", "sample"), "seq", "vocab"),
        P(("groups", "sample"), "seq", "vocab"),
        P(("groups", "sample"), "seq", "vocab"),
        P(("groups", "sample"), "seq", None),
        P("vocab", None),
        P(),
        P(("seq", "sample", "vocab"), None),
        P(("groups", "sample"), None),
        P(("groups", "sample"), None),
        P(("groups", "sample")),
        P(("groups", "sample")),
    )
    out_specs = (
        P(("groups", "sample"), "seq"),
        P(("groups", "sample")),
        P(("groups", "sample")),
        P("groups"),
    )
    body = functools.partial(shards, mesh.shape["seq"], mesh.shape["sample"])
    return jax.shard_map(body, mesh=mesh, in_specs=in_specs, out_specs=out_specs, check_vma=False)
```

time: 517 us -> 200 us (0.39)
  waiting for transfers between devices: 336 us -> 0 us
  Pallas kernels: 0 us -> 188 us
  blocking collectives: 71.2 us -> 0 us
  other arithmetic: 56.3 us -> 1.4 us
  between operations: 16.5 us -> 2.4 us
  matrix products: 13.3 us -> 0 us
  local copies, waits for them, and re-layouts: 17.8 us -> 7.94 us
    all_gather x3 -> x0, waiting for transfers between devices: 335 us -> none  [the longest x1 157 us: side_by_side(): lax.all_gather(both, axis, axis=dim, tiled=True)]
    pallas_call x0 -> x1, Pallas kernels: none -> 188 us  [shards(): pl.pallas_call(functools.partial(kernel, nz, nx, full_len), out_shape=(ja...]
    all_gather x1 -> x0, blocking collectives: 57 us -> none  [all_in_one(): both, at, found = (lax.all_gather(jnp.concatenate(lines), axis), 0, {})]
    add x65 -> x0, other arithmetic: 45.2 us -> none  [the longest x63 45.2 us: merge_stats(): left[1] * jnp.exp(left[0] - top_score)]
    dot_general x4 -> x0, matrix products: 13.3 us -> none  [the longest x1 8.49 us: shards(): lax.dot_general(flat, head_rows, (((1,), (1,)), ((), ())), preferred_elem...]
    gather x5 -> x0, local copies, waits for them, and re-layouts: 12.6 us -> none  [the longest x2 9.12 us: shards(): wanted = jnp.take_along_axis(targets, slot_piece, axis=1)]
    unnamed x1 -> x0, blocking collectives: 10.3 us -> none
  transfers between devices with their start and end apart: 3 -> 0, of which waited for: 3 -> 0; matrix products, arithmetic and copies ran while one was open for 5% -> 0% of each run, Pallas kernels for 0% -> 0%
where the time goes in v1:
time: 200 us
  Pallas kernels  188 us (94%)
  local copies, waits for them, and re-layouts  7.94 us (4%)
  between operations  2.4 us (1%)
    pallas_call x1, Pallas kernels, shards(): pl.pallas_call(functools.partial(kernel, nz, nx, full_len), out_shape=(ja...  188 us

profile of v1, /device:TPU:40, one launch (start us, length us, event | category | flops | bytes accessed | tf_op | source)
XLA Modules:
  0.0 200.0 jit_solution(1385425176798603964)
XLA Ops:
  0.6 0.8 reshape.38
  1.4 0.1 subtract_clamp_fusion
  1.5 0.8 broadcast_in_dim.17
  2.3 1.3 select_reduce_fusion
  3.6 0.8 stack_reshape.3
  4.4 0.1 copy.18
  4.5 0.1 copy.19
  4.5 0.6 pad.4.info_ref
  5.2 1.3 reshape.40.gain_ref
  6.4 188.3 %shard_map.138 = (f32[2,16]{1,0:T(2,128)}, f32[1,2]{1,0:T(1,128)}, f32[1,2]{1,0:T(1,128)}, f32[1,1]{1,0:T(1,128)}) custom-call(s32[32,1,128]{2,1,0:T(1,128)} %pad.4.info_ref, s32[2]{0:T(128)} %len_ref.1, s32[2]{0:T(128)} %rew_ref.1, f32[1,1792]{1,0:T(1,128)} %reshape.40.gain_ref, bf16[2,64,896]{2,1,0:T(8,128)(2,1)} %q_hbm.1, bf16[2,64,128]{2,1,0:T(8,128)(2,1)} %k_hbm.1, ...), custom_call_target="tpu_custom_call" | custom-call | tf_op jit(solution)/shard_map/pallas_call | solution.py:530
  194.7 1.2 copy.24
  195.9 1.2 copy.25
  197.1 1.1 copy.26
  (2 shorter events, 0.0 us)
